TPU v7x, 32 devices: a whole 2x2x4 slice. The times are simulated.
32 devices in a mesh: parts: 2 (over x), seq: 16 (over z, y, core).
Axes of the slice: x: 2, y: 2, z: 4, core: 2. Of those that a mesh axis runs over, the one named last changes fastest.
Arguments:
- tokens: bfloat16 [16384, 2560], P(('parts', 'seq')), parts along dimension 0, may hold values from -6 to 6
- lengths: int32 [32], P('parts'), parts along dimension 0, may hold values from 1 to 2048, 8192 in all
- gate_value_proj: bfloat16 [2560, 1280], replicated, may hold values from -0.125 to 0.125
- state_proj: bfloat16 [2560, 256], replicated, may hold values from -0.125 to 0.125
- step_proj: bfloat16 [2560, 10], replicated, may hold values from -0.125 to 0.125
- step_bias: float32 [10], replicated, may hold values from -3 to -1
- decay_log: float32 [10], replicated, may hold values from -8 to -1
- conv_weight: float32 [4, 896], replicated, may hold values from -3 to 3
- conv_bias: float32 [896], replicated, may hold values from -3 to 3
- skip_gain: float32 [10], replicated, may hold values from 0.5 to 2
- norm_gain: float32 [640], replicated, may hold values from 0.1 to 1.9
Outputs:
- normed: bfloat16 [16384, 640], P(('parts', 'seq')), parts along dimension 0
There are 2 independent parts, one for each index of `parts`. A program takes and returns all parts, laid end to end along the dimension named above; an argument that names none is the same for every part. Nothing has to cross between parts.
Inputs may be any that keep to these rules, and one draw needn't show every extreme that they name: The 16 lengths sum to 8192; the longest is exactly 2048.
All inputs are finite; a program needn't handle non-finite values.
Results may differ from a plain program's by a relative error of at most 0.0055.
Values may be sent and summed in bfloat16 or wider, within the bound.
A program may use at most 128 MiB of HBM per device.

v0:
```python
import functools

import jax
import jax.numpy as jnp
from jax import lax
from jax.experimental import pallas as pl
from jax.experimental.pallas import tpu as pltpu
from jax.sharding import PartitionSpec as P

CHUNK = 128
LANES = 128
HALO = 16
COLS = 256
MESH = pl.DeviceIdType.MESH
f32 = jnp.float32
bf16 = jnp.bfloat16


def split3(x):
    hi = x.astype(bf16)
    rest = x - hi.astype(f32)
    mid = rest.astype(bf16)
    return hi, mid, (rest - mid.astype(f32)).astype(bf16)


def expanded(x, spread):
    hi = x.astype(bf16)
    lo = (x - hi.astype(f32)).astype(bf16)
    return jnp.dot(jnp.concatenate([hi, lo], axis=1), spread, preferred_element_type=f32)


def half_silu(h):
    return h + h * jnp.tanh(h)


def kernel(
    n,
    span,
    tokens,
    lengths,
    gv_hbm,
    sp_hbm,
    stp_hbm,
    step_bias,
    decay_log,
    conv_weight,
    conv_bias,
    skip_gain,
    norm_gain,
    out,
    tok,
    gv,
    sp,
    stp,
    narrow,
    mixed,
    keep,
    conv,
    gate,
    ysum,
    enter,
    state32,
    state16,
    dec_mine,
    pair16,
    pair_dec,
    got_a,
    got_a_dec,
    got_b,
    got_b_dec,
    enter16,
    full16,
    load_sem,
    halo_sem,
    a_sem,
    b_send,
    b_recv,
    c_sem,
):
    rows = tokens.shape[0]
    inner = gate.shape[1]
    width = conv.shape[1]
    state = (width - inner) // 2
    half = state // 2
    heads = stp.shape[0]
    head = inner // heads
    docs = lengths.shape[0]
    chunks = rows // CHUNK
    me = lax.axis_index("seq")
    core = lax.rem(me, 2)
    mate = me + 1 - 2 * core
    first = me * rows

    blocks = list(range(0, 2 * inner, COLS))
    order = [b for b in blocks if b + COLS > inner] + [b for b in blocks if b + COLS <= inner]
    loads = {}

    def load(name, src, dst):
        loads[name] = pltpu.make_async_copy(src, dst, load_sem.at[len(loads)])
        loads[name].start()

    load("tok", tokens, tok.at[pl.ds(HALO, rows)])
    load("stp", stp_hbm, stp)
    load("sp", sp_hbm, sp)
    for b in order:
        load(b, gv_hbm.at[:, pl.ds(b, COLS)], gv.at[:, pl.ds(b, COLS)])

    offsets = [-1, 1] + [s * 2 * k for k in range(1, span + 1) for s in (-1, 1)]
    barrier = pltpu.get_barrier_semaphore()
    for o in offsets:
        @pl.when((me + o >= 0) & (me + o < n))
        def _(o=o):
            pl.semaphore_signal(barrier, inc=1, device_id={"seq": me + o}, device_id_type=MESH)
    peers = jnp.int32(0)
    for o in offsets:
        peers = peers + jnp.where((me + o >= 0) & (me + o < n), 1, 0)
    pl.semaphore_wait(barrier, peers)

    halo = pltpu.make_async_remote_copy(
        src_ref=tokens.at[pl.ds(rows - HALO, HALO)],
        dst_ref=tok.at[pl.ds(0, HALO)],
        send_sem=halo_sem.at[0],
        recv_sem=halo_sem.at[1],
        device_id={"seq": lax.rem(me + 1, n)},
        device_id_type=MESH,
    )

    @pl.when(me + 1 < n)
    def _():
        halo.start()

    @pl.when(me == 0)
    def _():
        tok[0:HALO, :] = jnp.zeros((HALO, tok.shape[1]), tok.dtype)

    starts = []
    total = jnp.int32(0)
    for j in range(docs):
        starts.append(total)
        total = total + lengths[j]
    pos = first + lax.broadcasted_iota(jnp.int32, (rows, LANES), 0)
    begin = jnp.zeros((rows, LANES), jnp.int32)
    for s in starts[1:]:
        begin = jnp.where(pos >= s, s, begin)

    def begin_of(p):
        b = jnp.int32(0)
        for s in starts[1:]:
            b = jnp.where(p >= s, s, b)
        return b

    for k in range(3):
        keep[k] = (pos - 3 + k >= begin).astype(f32)

    r = lax.broadcasted_iota(jnp.int32, (2 * LANES, inner), 0)
    c = lax.broadcasted_iota(jnp.int32, (2 * LANES, inner), 1)
    spread = (lax.rem(r, LANES) == c // head).astype(bf16)
    row_i = lax.broadcasted_iota(jnp.int32, (CHUNK, CHUNK), 0)
    col_i = lax.broadcasted_iota(jnp.int32, (CHUNK, CHUNK), 1)
    lower = (row_i >= col_i).astype(bf16)
    lower3 = jnp.concatenate([lower, lower, lower], axis=1)

    narrow[...] = jnp.zeros_like(narrow)
    loads["tok"].wait()
    loads["stp"].wait()
    own = tok.at[pl.ds(HALO, rows)]
    raw = lax.dot_general(
        own[...], stp[...], (((1,), (1,)), ((), ())), preferred_element_type=f32
    )
    narrow[0:rows, 0:heads] = raw
    narrow[rows : rows + 1, 0:heads] = step_bias[...]
    narrow[rows + 8 : rows + 9, 0:heads] = decay_log[...]
    narrow[rows + 16 : rows + 17, 0:heads] = skip_gain[...]
    live = lax.broadcasted_iota(jnp.int32, (rows, LANES), 1) < heads
    shifted = narrow[0:rows, :] + narrow[rows : rows + 1, :]
    step = jnp.maximum(shifted, 0.0) + jnp.log1p(jnp.exp(-jnp.abs(shifted)))
    step = jnp.where(live, step, 0.0)
    log_decay = -step * jnp.exp(narrow[rows + 8 : rows + 9, :])
    skip_row = expanded(narrow[rows + 16 : rows + 24, :], spread)[0:1]
    hi, mid, lo = split3(log_decay)
    cums, cums_t, steps_t, leaving, entering = [], [], [], [], []
    for ch in range(chunks):
        at = slice(ch * CHUNK, (ch + 1) * CHUNK)
        cum = jnp.dot(
            lower3,
            jnp.concatenate([hi[at], mid[at], lo[at]], axis=0),
            preferred_element_type=f32,
        )
        cums.append(cum)
        cums_t.append(cum.T)
        steps_t.append(step[at].T)
        chunk_first = first + ch * CHUNK
        last_begin = begin_of(chunk_first + CHUNK - 1)
        leaving.append(
            jnp.where(
                pos[at] >= last_begin, jnp.exp(cum[CHUNK - 1 : CHUNK] - cum), 0.0
            )
            * step[at]
        )
        entering.append(jnp.where(begin[at] < chunk_first, jnp.exp(cum), 0.0))
    leave_wide = []
    for ch in range(chunks):
        at = slice(ch * CHUNK, (ch + 1) * CHUNK)
        leave_wide.append(expanded(leaving[ch], spread))
        enter[at, :] = expanded(entering[ch], spread)

    bias_row = 0.5 * conv_bias[...].reshape(1, width)
    gain_row = norm_gain[...].reshape(1, inner)

    def convolve(lo_col, count):
        cols = slice(lo_col, lo_col + count)
        w = 0.5 * conv_weight[:, cols]
        h = bias_row[:, cols] + w[3:4] * mixed[HALO : HALO + rows, cols]
        for k in range(3):
            kept = keep[k]
            if count != LANES:
                kept = jnp.concatenate([kept] * (count // LANES), axis=1)
            h = h + w[k : k + 1] * (
                kept * mixed[HALO - 3 + k : HALO - 3 + k + rows, cols]
            )
        conv[:, cols] = half_silu(h).astype(bf16)

    @pl.when(me > 0)
    def _():
        halo.wait_recv()

    loads["sp"].wait()
    both = jnp.dot(tok[...], sp[...], preferred_element_type=f32)
    mixed[:, inner:width] = both.astype(bf16).astype(f32)
    pending = [(inner, width - inner)]
    for b in order:
        if b + COLS <= inner:
            continue
        loads[b].wait()
        got = jnp.dot(tok[...], gv[:, b : b + COLS], preferred_element_type=f32)
        got = got.astype(bf16).astype(f32)
        gates = max(0, inner - b)
        if gates:
            gate[:, b:inner] = half_silu(0.5 * got[HALO:, :gates])
        mixed[:, b + gates - inner : b + COLS - inner] = got[:, gates:]
        for p in pending:
            convolve(*p)
        pending = [(b + gates - inner, COLS - gates)]
    for p in pending:
        convolve(*p)

    locals_ = []
    for ch in range(chunks):
        at = slice(ch * CHUNK, (ch + 1) * CHUNK)
        weighted = (conv[at, 0:inner].astype(f32) * leave_wide[ch]).astype(bf16)
        locals_.append(
            lax.dot_general(
                conv[at, inner : inner + state],
                weighted,
                (((0,), (0,)), ((), ())),
                preferred_element_type=f32,
            )
        )
    decs = [enter[(ch + 1) * CHUNK - 1 : (ch + 1) * CHUNK, :] for ch in range(chunks)]
    device_state = locals_[0]
    device_dec = decs[0]
    for ch in range(1, chunks):
        device_state = decs[ch] * device_state + locals_[ch]
        device_dec = decs[ch] * device_dec
    for ch in range(chunks):
        state32[ch] = locals_[ch]
    state32[chunks] = device_state
    state16[...] = device_state.astype(bf16)

    def put_row(ref, row):
        for j in range(inner // LANES):
            ref[j : j + 1, :] = row[:, j * LANES : (j + 1) * LANES]

    def get_row(block):
        return jnp.concatenate([block[j : j + 1] for j in range(inner // LANES)], axis=1)

    put_row(dec_mine, device_dec)
    mine_at = pl.multiple_of(core * half, half)
    mate_at = pl.multiple_of((1 - core) * half, half)

    def remote(src, dst, send, recv, target):
        return pltpu.make_async_remote_copy(
            src_ref=src,
            dst_ref=dst,
            send_sem=send,
            recv_sem=recv,
            device_id={"seq": target},
            device_id_type=MESH,
        )

    a_copy = remote(state16.at[pl.ds(mate_at, half)], got_a, a_sem.at[0], a_sem.at[1], mate)
    a_dec = remote(dec_mine, got_a_dec, a_sem.at[2], a_sem.at[3], mate)
    a_copy.start()
    a_dec.start()

    def inside(ch):
        at = slice(ch * CHUNK, (ch + 1) * CHUNK)
        in_map = conv[at, inner : inner + state]
        out_map = conv[at, inner + state : width]
        scores = lax.dot_general(
            out_map, in_map, (((1,), (1,)), ((), ())), preferred_element_type=f32
        )
        allowed = (row_i >= col_i) & (first + ch * CHUNK + col_i >= begin[at])
        lane = lax.broadcasted_iota(jnp.int32, (CHUNK, LANES), 1)
        per = LANES // head
        for tile in range(inner // LANES):
            x = conv[at, tile * LANES : (tile + 1) * LANES]
            mixes, values = [], []
            for i in range(per):
                h = tile * per + i
                diff = jnp.minimum(cums[ch][:, h : h + 1] - cums_t[ch][h : h + 1, :], 0.0)
                weight = jnp.where(allowed, jnp.exp(diff), 0.0)
                mixes.append((weight * scores * steps_t[ch][h : h + 1, :]).astype(bf16))
                values.append(jnp.where(lane // head == i, x, jnp.zeros_like(x)))
            y = jnp.dot(
                jnp.concatenate(mixes, axis=1),
                jnp.concatenate(values, axis=0),
                preferred_element_type=f32,
            )
            cols = slice(tile * LANES, (tile + 1) * LANES)
            ysum[at, cols] = y + skip_row[:, cols] * x.astype(f32)

    inside(0)

    a_copy.wait()
    a_dec.wait()
    theirs = got_a[...].astype(f32)
    theirs_dec = get_row(got_a_dec[...])
    mine = state32[chunks, pl.ds(mine_at, half), :]
    even = core == 0
    early = jnp.where(even, mine, theirs)
    early_dec = jnp.where(even, device_dec, theirs_dec)
    late = jnp.where(even, theirs, mine)
    late_dec = jnp.where(even, theirs_dec, device_dec)
    pair16[...] = (late + late_dec * early).astype(bf16)
    put_row(pair_dec, late_dec * early_dec)

    b_copies = []
    for k in range(1, span + 1):
        target = lax.rem(me + 2 * k, n)
        b_copies.append(
            (
                remote(pair16, got_b.at[k - 1], b_send.at[2 * k - 2], b_recv.at[2 * k - 2], target),
                remote(
                    pair_dec, got_b_dec.at[k - 1], b_send.at[2 * k - 1], b_recv.at[2 * k - 1], target
                ),
            )
        )
    for k in range(1, span + 1):
        @pl.when(me + 2 * k < n)
        def _(k=k):
            for cp in b_copies[k - 1]:
                cp.start()

        @pl.when(me - 2 * k < 0)
        def _(k=k):
            got_b[k - 1] = jnp.zeros(got_b.shape[1:], bf16)
            got_b_dec[k - 1] = jnp.zeros(got_b_dec.shape[1:], f32)

    for b in order:
        if b + COLS > inner:
            continue
        loads[b].wait()
        got = jnp.dot(own[...], gv[:, b : b + COLS], preferred_element_type=f32)
        gate[:, b : b + COLS] = half_silu(0.5 * got.astype(bf16).astype(f32))
    for ch in range(1, chunks):
        inside(ch)

    for k in range(1, span + 1):
        @pl.when(me - 2 * k >= 0)
        def _(k=k):
            for cp in b_copies[k - 1]:
                cp.wait_recv()
    chip = jnp.zeros((half, inner), f32)
    for k in range(span, 0, -1):
        chip = got_b[k - 1].astype(f32) + get_row(got_b_dec[k - 1]) * chip
    second = early + early_dec * chip
    full16[pl.ds(mine_at, half), :] = jnp.where(even, chip, second).astype(bf16)
    enter16[...] = jnp.where(even, second, chip).astype(bf16)
    c_copy = remote(enter16, full16.at[pl.ds(mine_at, half)], c_sem.at[0], c_sem.at[1], mate)
    c_copy.start()
    c_copy.wait()

    carried = full16[...].astype(f32)
    for ch in range(chunks):
        at = slice(ch * CHUNK, (ch + 1) * CHUNK)
        off = jnp.dot(
            conv[at, inner + state : width], carried.astype(bf16), preferred_element_type=f32
        )
        gated = (ysum[at, :] + enter[at, :] * off) * gate[at, :]
        square = jnp.sum(gated * gated, axis=1, keepdims=True) * (1.0 / inner)
        out[at, :] = (gated * lax.rsqrt(square + 1e-05) * gain_row).astype(bf16)
        if ch + 1 < chunks:
            carried = decs[ch] * carried + state32[ch]

    @pl.when(me + 1 < n)
    def _():
        halo.wait_send()

    for k in range(1, span + 1):
        @pl.when(me + 2 * k < n)
        def _(k=k):
            for cp in b_copies[k - 1]:
                cp.wait_send()


def shards(
    tokens,
    lengths,
    gate_value_proj,
    state_proj,
    step_proj,
    step_bias,
    decay_log,
    conv_weight,
    conv_bias,
    skip_gain,
    norm_gain,
):
    rows, depth = tokens.shape
    inner = gate_value_proj.shape[1] // 2
    state = state_proj.shape[1] // 2
    heads = step_proj.shape[1]
    width = inner + 2 * state
    n = lax.axis_size("seq")
    span = max(1, n // 8)
    hbm = pl.BlockSpec(memory_space=pl.ANY)
    vmem = pl.BlockSpec(memory_space=pltpu.VMEM)
    half = state // 2
    small = (8, LANES)
    chunks = rows // CHUNK
    dma = pltpu.SemaphoreType.DMA
    blocks = 2 * inner // COLS
    return pl.pallas_call(
        functools.partial(kernel, n, span),
        out_shape=jax.ShapeDtypeStruct((rows, inner), bf16),
        in_specs=[hbm, pl.BlockSpec(memory_space=pltpu.SMEM), hbm, hbm, hbm] + [vmem] * 6,
        out_specs=vmem,
        scratch_shapes=[
            pltpu.VMEM((rows + HALO, depth), bf16),
            pltpu.VMEM((depth, 2 * inner), bf16),
            pltpu.VMEM((depth, 2 * state), bf16),
            pltpu.VMEM((heads, depth), bf16),
            pltpu.VMEM((rows + 24, LANES), f32),
            pltpu.VMEM((rows + HALO, width), f32),
            pltpu.VMEM((3, rows, LANES), f32),
            pltpu.VMEM((rows, width), bf16),
            pltpu.VMEM((rows, inner), f32),
            pltpu.VMEM((rows, inner), f32),
            pltpu.VMEM((rows, inner), f32),
            pltpu.VMEM((chunks + 1, state, inner), f32),
            pltpu.VMEM((state, inner), bf16),
            pltpu.VMEM(small, f32),
            pltpu.VMEM((half, inner), bf16),
            pltpu.VMEM(small, f32),
            pltpu.VMEM((half, inner), bf16),
            pltpu.VMEM(small, f32),
            pltpu.VMEM((span, half, inner), bf16),
            pltpu.VMEM((span,) + small, f32),
            pltpu.VMEM((half, inner), bf16),
            pltpu.VMEM((state, inner), bf16),
            dma((3 + blocks,)),
            dma((2,)),
            dma((4,)),
            dma((2 * span,)),
            dma((2 * span,)),
            dma((2,)),
        ],
        compiler_params=pltpu.CompilerParams(
            collective_id=0, has_side_effects=True, vmem_limit_bytes=60 * 1024 * 1024
        ),
        name="layer",
    )(
        tokens,
        lengths,
        gate_value_proj,
        state_proj,
        step_proj.T,
        step_bias[None],
        decay_log[None],
        conv_weight,
        conv_bias,
        skip_gain[None],
        norm_gain,
    )


def solution(mesh):
    return jax.shard_map(
        shards,
        mesh=mesh,
        in_specs=(P(("parts", "seq"), None), P("parts")) + (P(),) * 9,
        out_specs=P(("parts", "seq"), None),
        check_vma=False,
    )
```

profile of v0, /device:TPU:21, one launch (start us, length us, event | category | flops | bytes accessed | tf_op | source)
XLA Modules:
  0.0 24.4 jit_solution(12687755544884312986)
XLA Ops:
  0.0 22.4 %layer.1 = bf16[512,640]{1,0:T(8,128)(2,1)} custom-call(bf16[512,2560]{1,0:T(8,128)(2,1)} %tokens.1, s32[16]{0:T(128)} %lengths.1, bf16[2560,1280]{1,0:T(8,128)(2,1)} %gv_hbm.1, bf16[2560,256]{1,0:T(8,128)(2,1)} %sp_hbm.1, bf16[10,2560]{1,0:T(8,128)(2,1)} %bitcast.4, f32[1,10]{1,0:T(1,128)} %bitcast.5, f32[1,10]{1,0:T(1,128)} %bitcast.6, ...), custom_call_target="tpu_custom_call" | custom-call | tf_op jit(solution)/shard_map/layer/pallas_call | solution.py:434
  22.4 2.0 %copy.13 = bf16[512,640]{1,0:T(8,128)(2,1)} copy(bf16[512,640]{1,0:T(8,128)(2,1)} %layer.1) | data formatting | bytes 1310720
where the time goes:
time: 24.6 us; the launch traced here: 24.4 us
  Pallas kernels  22.4 us (91%)
  local copies, waits for them, and re-layouts  1.98 us (8%)
    pallas_call x1, Pallas kernels, shards(): pl.pallas_call(functools.partial(kernel, n, span), out_shape=jax.ShapeDty...  22.4 us
    unnamed x1, local copies, waits for them, and re-layouts  1.98 us

commit v1 on v0

--- a/solution.py
+++ b/solution.py
@@ -37,17 +37,25 @@
     n,
     span,
     tokens,
-    lengths,
+    lengths_hbm,
     gv_hbm,
     sp_hbm,
     stp_hbm,
+    step_bias_hbm,
+    decay_log_hbm,
+    conv_weight_hbm,
+    conv_bias_hbm,
+    skip_gain_hbm,
+    norm_gain_hbm,
+    out,
+    lengths,
     step_bias,
     decay_log,
     conv_weight,
     conv_bias,
     skip_gain,
     norm_gain,
-    out,
+    leave,
     tok,
     gv,
     sp,
@@ -92,15 +100,29 @@
     first = me * rows
 
     blocks = list(range(0, 2 * inner, COLS))
-    order = [b for b in blocks if b + COLS > inner] + [b for b in blocks if b + COLS <= inner]
+    order = [b for b in blocks if b >= inner]
+    order += [b for b in blocks if b < inner < b + COLS]
+    order += [b for b in blocks if b + COLS <= inner]
     loads = {}
 
     def load(name, src, dst):
         loads[name] = pltpu.make_async_copy(src, dst, load_sem.at[len(loads)])
         loads[name].start()
 
+    load("lengths", lengths_hbm, lengths)
+    load("stp", stp_hbm, stp)
     load("tok", tokens, tok.at[pl.ds(HALO, rows)])
-    load("stp", stp_hbm, stp)
+    smalls = [
+        (step_bias_hbm, step_bias),
+        (decay_log_hbm, decay_log),
+        (skip_gain_hbm, skip_gain),
+        (conv_weight_hbm, conv_weight),
+    ]
+    for src, dst in ((conv_bias_hbm, conv_bias), (norm_gain_hbm, norm_gain)):
+        for i in range(0, src.shape[0], LANES):
+            smalls.append((src.at[pl.ds(i, LANES)], dst.at[pl.ds(i, LANES)]))
+    for i, (src, dst) in enumerate(smalls):
+        load(("small", i), src, dst)
     load("sp", sp_hbm, sp)
     for b in order:
         load(b, gv_hbm.at[:, pl.ds(b, COLS)], gv.at[:, pl.ds(b, COLS)])
@@ -133,6 +155,7 @@
     def _():
         tok[0:HALO, :] = jnp.zeros((HALO, tok.shape[1]), tok.dtype)
 
+    loads["lengths"].wait()
     starts = []
     total = jnp.int32(0)
     for j in range(docs):
@@ -161,8 +184,10 @@
     lower3 = jnp.concatenate([lower, lower, lower], axis=1)
 
     narrow[...] = jnp.zeros_like(narrow)
+    for i in range(len(smalls)):
+        loads["small", i].wait()
+    loads["stp"].wait()
     loads["tok"].wait()
-    loads["stp"].wait()
     own = tok.at[pl.ds(HALO, rows)]
     raw = lax.dot_general(
         own[...], stp[...], (((1,), (1,)), ((), ())), preferred_element_type=f32
@@ -171,55 +196,6 @@
     narrow[rows : rows + 1, 0:heads] = step_bias[...]
     narrow[rows + 8 : rows + 9, 0:heads] = decay_log[...]
     narrow[rows + 16 : rows + 17, 0:heads] = skip_gain[...]
-    live = lax.broadcasted_iota(jnp.int32, (rows, LANES), 1) < heads
-    shifted = narrow[0:rows, :] + narrow[rows : rows + 1, :]
-    step = jnp.maximum(shifted, 0.0) + jnp.log1p(jnp.exp(-jnp.abs(shifted)))
-    step = jnp.where(live, step, 0.0)
-    log_decay = -step * jnp.exp(narrow[rows + 8 : rows + 9, :])
-    skip_row = expanded(narrow[rows + 16 : rows + 24, :], spread)[0:1]
-    hi, mid, lo = split3(log_decay)
-    cums, cums_t, steps_t, leaving, entering = [], [], [], [], []
-    for ch in range(chunks):
-        at = slice(ch * CHUNK, (ch + 1) * CHUNK)
-        cum = jnp.dot(
-            lower3,
-            jnp.concatenate([hi[at], mid[at], lo[at]], axis=0),
-            preferred_element_type=f32,
-        )
-        cums.append(cum)
-        cums_t.append(cum.T)
-        steps_t.append(step[at].T)
-        chunk_first = first + ch * CHUNK
-        last_begin = begin_of(chunk_first + CHUNK - 1)
-        leaving.append(
-            jnp.where(
-                pos[at] >= last_begin, jnp.exp(cum[CHUNK - 1 : CHUNK] - cum), 0.0
-            )
-            * step[at]
-        )
-        entering.append(jnp.where(begin[at] < chunk_first, jnp.exp(cum), 0.0))
-    leave_wide = []
-    for ch in range(chunks):
-        at = slice(ch * CHUNK, (ch + 1) * CHUNK)
-        leave_wide.append(expanded(leaving[ch], spread))
-        enter[at, :] = expanded(entering[ch], spread)
-
-    bias_row = 0.5 * conv_bias[...].reshape(1, width)
-    gain_row = norm_gain[...].reshape(1, inner)
-
-    def convolve(lo_col, count):
-        cols = slice(lo_col, lo_col + count)
-        w = 0.5 * conv_weight[:, cols]
-        h = bias_row[:, cols] + w[3:4] * mixed[HALO : HALO + rows, cols]
-        for k in range(3):
-            kept = keep[k]
-            if count != LANES:
-                kept = jnp.concatenate([kept] * (count // LANES), axis=1)
-            h = h + w[k : k + 1] * (
-                kept * mixed[HALO - 3 + k : HALO - 3 + k + rows, cols]
-            )
-        conv[:, cols] = half_silu(h).astype(bf16)
-
     @pl.when(me > 0)
     def _():
         halo.wait_recv()
@@ -227,45 +203,93 @@
     loads["sp"].wait()
     both = jnp.dot(tok[...], sp[...], preferred_element_type=f32)
     mixed[:, inner:width] = both.astype(bf16).astype(f32)
+
+    live = lax.broadcasted_iota(jnp.int32, (CHUNK, LANES), 1) < heads
+    rate = jnp.exp(narrow[rows + 8 : rows + 9, :])
+    skip_row = expanded(narrow[rows + 16 : rows + 24, :], spread)[0:1]
+    cums, cums_t, steps_t = [], [], []
+    for ch in range(chunks):
+        at = slice(ch * CHUNK, (ch + 1) * CHUNK)
+        shifted = narrow[at, :] + narrow[rows : rows + 1, :]
+        step = jnp.maximum(shifted, 0.0) + jnp.log1p(jnp.exp(-jnp.abs(shifted)))
+        step = jnp.where(live, step, 0.0)
+        cum = jnp.dot(
+            lower3, jnp.concatenate(split3(-step * rate), axis=0), preferred_element_type=f32
+        )
+        cums.append(cum)
+        cums_t.append(cum.T)
+        steps_t.append(step.T)
+        chunk_first = first + ch * CHUNK
+        last_begin = begin_of(chunk_first + CHUNK - 1)
+        here = first + ch * CHUNK + row_i
+        leave[at, :] = (
+            jnp.where(here >= last_begin, jnp.exp(cum[CHUNK - 1 : CHUNK] - cum), 0.0) * step
+        )
+        reach = jnp.where(begin[at] < chunk_first, jnp.exp(cum), 0.0)
+        enter[at, 0:LANES] = reach
+        narrow[rows + 24 + ch : rows + 25 + ch, :] = reach[CHUNK - 1 : CHUNK]
+    wide_decs = expanded(narrow[rows + 24 : rows + 24 + 8 * ((chunks + 7) // 8), :], spread)
+    decs = [wide_decs[ch : ch + 1] for ch in range(chunks)]
+
+    bias_row = 0.5 * conv_bias[0:width].reshape(1, width)
+    gain_row = norm_gain[0:inner].reshape(1, inner)
+
+    piece = 64
+
+    def convolve(lo_col, count):
+        for col in range(lo_col, lo_col + count, LANES):
+            cols = slice(col, col + LANES)
+            w = 0.5 * conv_weight[:, cols]
+            bias = bias_row[:, cols]
+            for at in range(0, rows, piece):
+                h = bias + w[3:4] * mixed[HALO + at : HALO + at + piece, cols]
+                for k in range(3):
+                    low = HALO - 3 + k + at
+                    h = h + w[k : k + 1] * (
+                        keep[k, at : at + piece, :] * mixed[low : low + piece, cols]
+                    )
+                conv[at : at + piece, cols] = half_silu(h).astype(bf16)
+
+    def states(lo_col, count):
+        cols = slice(lo_col, lo_col + count)
+        total = None
+        for ch in range(chunks):
+            at = slice(ch * CHUNK, (ch + 1) * CHUNK)
+            weighted = conv[at, cols].astype(f32) * expanded(leave[at, :], spread[:, cols])
+            own_state = lax.dot_general(
+                conv[at, inner : inner + state],
+                weighted.astype(bf16),
+                (((0,), (0,)), ((), ())),
+                preferred_element_type=f32,
+            )
+            state32[ch, :, cols] = own_state
+            total = own_state if ch == 0 else decs[ch][:, cols] * total + own_state
+        state32[chunks, :, cols] = total
+        state16[:, cols] = total.astype(bf16)
+
     pending = [(inner, width - inner)]
     for b in order:
         if b + COLS <= inner:
             continue
         loads[b].wait()
         got = jnp.dot(tok[...], gv[:, b : b + COLS], preferred_element_type=f32)
-        got = got.astype(bf16).astype(f32)
         gates = max(0, inner - b)
         if gates:
-            gate[:, b:inner] = half_silu(0.5 * got[HALO:, :gates])
-        mixed[:, b + gates - inner : b + COLS - inner] = got[:, gates:]
+            gate[:, b:inner] = 0.5 * got[HALO:, :gates].astype(bf16).astype(f32)
+        mixed[:, b + gates - inner : b + COLS - inner] = (
+            got[:, gates:].astype(bf16).astype(f32)
+        )
         for p in pending:
             convolve(*p)
+            if p[0] < inner:
+                states(*p)
         pending = [(b + gates - inner, COLS - gates)]
     for p in pending:
         convolve(*p)
-
-    locals_ = []
-    for ch in range(chunks):
-        at = slice(ch * CHUNK, (ch + 1) * CHUNK)
-        weighted = (conv[at, 0:inner].astype(f32) * leave_wide[ch]).astype(bf16)
-        locals_.append(
-            lax.dot_general(
-                conv[at, inner : inner + state],
-                weighted,
-                (((0,), (0,)), ((), ())),
-                preferred_element_type=f32,
-            )
-        )
-    decs = [enter[(ch + 1) * CHUNK - 1 : (ch + 1) * CHUNK, :] for ch in range(chunks)]
-    device_state = locals_[0]
+        states(*p)
     device_dec = decs[0]
     for ch in range(1, chunks):
-        device_state = decs[ch] * device_state + locals_[ch]
         device_dec = decs[ch] * device_dec
-    for ch in range(chunks):
-        state32[ch] = locals_[ch]
-    state32[chunks] = device_state
-    state16[...] = device_state.astype(bf16)
 
     def put_row(ref, row):
         for j in range(inner // LANES):
@@ -320,6 +344,10 @@
             cols = slice(tile * LANES, (tile + 1) * LANES)
             ysum[at, cols] = y + skip_row[:, cols] * x.astype(f32)
 
+    def widen(ch):
+        at = slice(ch * CHUNK, (ch + 1) * CHUNK)
+        enter[at, :] = expanded(enter[at, 0:LANES], spread)
+
     inside(0)
 
     a_copy.wait()
@@ -362,9 +390,13 @@
             continue
         loads[b].wait()
         got = jnp.dot(own[...], gv[:, b : b + COLS], preferred_element_type=f32)
-        gate[:, b : b + COLS] = half_silu(0.5 * got.astype(bf16).astype(f32))
+        gate[:, b : b + COLS] = 0.5 * got.astype(bf16).astype(f32)
     for ch in range(1, chunks):
         inside(ch)
+    for ch in range(chunks):
+        at = slice(ch * CHUNK, (ch + 1) * CHUNK)
+        widen(ch)
+        gate[at, :] = half_silu(gate[at, :])
 
     for k in range(1, span + 1):
         @pl.when(me - 2 * k >= 0)
@@ -434,14 +466,22 @@
     return pl.pallas_call(
         functools.partial(kernel, n, span),
         out_shape=jax.ShapeDtypeStruct((rows, inner), bf16),
-        in_specs=[hbm, pl.BlockSpec(memory_space=pltpu.SMEM), hbm, hbm, hbm] + [vmem] * 6,
+        in_specs=[hbm] * 11,
         out_specs=vmem,
         scratch_shapes=[
+            pltpu.SMEM(lengths.shape, jnp.int32),
+            pltpu.VMEM((1, heads), f32),
+            pltpu.VMEM((1, heads), f32),
+            pltpu.VMEM(conv_weight.shape, f32),
+            pltpu.VMEM((1024 * pl.cdiv(width, 1024),), f32),
+            pltpu.VMEM((1, heads), f32),
+            pltpu.VMEM((1024 * pl.cdiv(inner, 1024),), f32),
+            pltpu.VMEM((rows, LANES), f32),
             pltpu.VMEM((rows + HALO, depth), bf16),
             pltpu.VMEM((depth, 2 * inner), bf16),
             pltpu.VMEM((depth, 2 * state), bf16),
             pltpu.VMEM((heads, depth), bf16),
-            pltpu.VMEM((rows + 24, LANES), f32),
+            pltpu.VMEM((rows + 24 + 8 * ((chunks + 7) // 8), LANES), f32),
             pltpu.VMEM((rows + HALO, width), f32),
             pltpu.VMEM((3, rows, LANES), f32),
             pltpu.VMEM((rows, width), bf16),
@@ -459,7 +499,7 @@
             pltpu.VMEM((span,) + small, f32),
             pltpu.VMEM((half, inner), bf16),
             pltpu.VMEM((state, inner), bf16),
-            dma((3 + blocks,)),
+            dma((8 + blocks + (width + inner) // LANES,)),
             dma((2,)),
             dma((4,)),
             dma((2 * span,)),

time: 24.6 us -> 23.5 us (0.955)
  Pallas kernels: 22.4 us -> 21.4 us
    pallas_call x1, Pallas kernels: 22.4 us -> 21.4 us  [shards(): pl.pallas_call(functools.partial(kernel, n, span), out_shape=jax.ShapeDty...]
where the time goes in v1:
time: 23.5 us; the launch traced here: 23.3 us
  Pallas kernels  21.4 us (91%)
  local copies, waits for them, and re-layouts  1.98 us (8%)
    pallas_call x1, Pallas kernels, shards(): pl.pallas_call(functools.partial(kernel, n, span), out_shape=jax.ShapeDty...  21.4 us
    unnamed x1, local copies, waits for them, and re-layouts  1.98 us

profile of v1, /device:TPU:21, one launch (start us, length us, event | category | flops | bytes accessed | tf_op | source)
XLA Modules:
  0.0 23.3 jit_solution(3123851190079222672)
XLA Ops:
  0.0 21.4 %layer.1 = bf16[512,640]{1,0:T(8,128)(2,1)} custom-call(bf16[512,2560]{1,0:T(8,128)(2,1)} %tokens.1, s32[16]{0:T(128)} %lengths_hbm.1, bf16[2560,1280]{1,0:T(8,128)(2,1)} %gv_hbm.1, bf16[2560,256]{1,0:T(8,128)(2,1)} %sp_hbm.1, bf16[10,2560]{1,0:T(8,128)(2,1)} %bitcast.4, f32[1,10]{1,0:T(1,128)} %bitcast.5, f32[1,10]{1,0:T(1,128)} %bitcast.6, ...), custom_call_target="tpu_custom_call" | custom-call | tf_op jit(solution)/shard_map/layer/pallas_call | solution.py:466
  21.4 2.0 %copy.13 = bf16[512,640]{1,0:T(8,128)(2,1)} copy(bf16[512,640]{1,0:T(8,128)(2,1)} %layer.1) | data formatting | bytes 1310720

commit v2 on v1

--- a/solution.py
+++ b/solution.py
@@ -456,7 +456,7 @@
     width = inner + 2 * state
     n = lax.axis_size("seq")
     span = max(1, n // 8)
-    hbm = pl.BlockSpec(memory_space=pl.ANY)
+    hbm = pl.BlockSpec(memory_space=pltpu.HBM)
     vmem = pl.BlockSpec(memory_space=pltpu.VMEM)
     half = state // 2
     small = (8, LANES)
@@ -465,7 +465,7 @@
     blocks = 2 * inner // COLS
     return pl.pallas_call(
         functools.partial(kernel, n, span),
-        out_shape=jax.ShapeDtypeStruct((rows, inner), bf16),
+        out_shape=pltpu.VMEM((rows, inner), bf16),
         in_specs=[hbm] * 11,
         out_specs=vmem,
         scratch_shapes=[
@@ -507,7 +507,7 @@
             dma((2,)),
         ],
         compiler_params=pltpu.CompilerParams(
-            collective_id=0, has_side_effects=True, vmem_limit_bytes=60 * 1024 * 1024
+            collective_id=0, has_side_effects=True, vmem_limit_bytes=66_000_000
         ),
         name="layer",
     )(

time: 23.5 us -> 21.5 us (0.915)
  local copies, waits for them, and re-layouts: 1.98 us -> 0.84 us
  Pallas kernels: 21.4 us -> 20.5 us
    unnamed x1, local copies, waits for them, and re-layouts: 1.98 us -> 0.84 us
    pallas_call x1, Pallas kernels: 21.4 us -> 20.5 us  [shards(): pl.pallas_call(functools.partial(kernel, n, span), out_shape=pltpu.VMEM((...]
where the time goes in v2:
time: 21.5 us; the launch traced here: 21.4 us
  Pallas kernels  20.5 us (95%)
  local copies, waits for them, and re-layouts  0.84 us (4%)
    pallas_call x1, Pallas kernels, shards(): pl.pallas_call(functools.partial(kernel, n, span), out_shape=pltpu.VMEM((...  20.5 us
    unnamed x1, local copies, waits for them, and re-layouts  0.84 us

profile of v2, /device:TPU:21, one launch (start us, length us, event | category | flops | bytes accessed | tf_op | source)
XLA Modules:
  0.0 21.4 jit_solution(5810584227941572785)
XLA Ops:
  0.0 20.5 %layer.1 = bf16[512,640]{1,0:T(8,128)(2,1)S(1)} custom-call(bf16[512,2560]{1,0:T(8,128)(2,1)} %tokens.1, s32[16]{0:T(128)} %lengths_hbm.1, bf16[2560,1280]{1,0:T(8,128)(2,1)} %gv_hbm.1, bf16[2560,256]{1,0:T(8,128)(2,1)} %sp_hbm.1, bf16[10,2560]{1,0:T(8,128)(2,1)} %bitcast.4, f32[1,10]{1,0:T(1,128)} %bitcast.5, f32[1,10]{1,0:T(1,128)} %bitcast.6, ...), custom_call_target="tpu_custom_call" | custom-call | tf_op jit(solution)/shard_map/layer/pallas_call | solution.py:466
  20.5 0.8 %copy.13 = bf16[512,640]{1,0:T(8,128)(2,1)} copy(bf16[512,640]{1,0:T(8,128)(2,1)S(1)} %layer.1) | data formatting | bytes 1310720
